TPU v7x, 32 devices: a whole 2x2x4 slice. The times are simulated.
32 devices in a mesh: rows: 8 (over z, y), protos: 4 (over x, core).
Axes of the slice: x: 2, y: 2, z: 4, core: 2. Of those that a mesh axis runs over, the one named last changes fastest.
Arguments:
- features: bfloat16 [3072, 256], P('rows', 'protos'), may hold values from -12 to 12
- prototypes: bfloat16 [65536, 256], P('protos', 'rows'), may hold values from -8 to 8
- masked_index: int32 [1536], P('rows'), may hold values from 0 to 383
Outputs:
- targets: bfloat16 [1536, 65536], P('rows', 'protos')
Inputs may be any that keep to these rules, and one draw needn't show every extreme that they name: Row r of the whole takes patch (r // 192) * 384 + masked_index[r] of features.
All inputs are finite; a program needn't handle non-finite values.
Results may differ from a plain program's by a relative error of at most 0.001.
Values may be sent and summed in bfloat16 or wider, within the bound.
A program may use at most 64 MiB of HBM per device.

v0:
```python
import functools

import jax
import jax.numpy as jnp
from jax import lax
from jax.experimental import pallas as pl
from jax.experimental.pallas import tpu as pltpu
from jax.sharding import PartitionSpec as P

ITERS = 3


TEMP = 0.07
EPS = 1e-06
UP, DOWN, ACROSS = 0, 1, 2
LEAD = 2
SPLIT = 1


def kernel(
    n_rows, n_protos, masked, protos_all,
    feat_ref, proto_ref, index_ref, weights, rs_ref, cs_ref,
    feat_full, index, onehot, full, chosen, feat_scale, acc, parts, masses, row_out, row_in,
    feat_send, feat_recv, in_sem, own_sem, send, recv,
    mass_send, mass_recv, scale_send, scale_recv, row_send, row_recv,
):
    r, p = lax.axis_index("rows"), lax.axis_index("protos")
    z, y = r // 2, lax.rem(r, 2)
    nz = n_rows // 2
    other = 1 - y
    dim, total = proto_ref.shape
    width = total // n_rows
    chunks = n_rows * SPLIT
    span = total // chunks
    rows = weights.shape[0]
    fdim = feat_ref.shape[0]
    tile = min(512, span)
    tiles = width // tile
    mesh_id = pl.DeviceIdType.MESH

    barrier = pltpu.get_barrier_semaphore()
    for step in range(1, n_rows):
        pl.semaphore_signal(
            barrier, inc=1, device_id={"rows": lax.rem(r + step, n_rows)}, device_id_type=mesh_id
        )
    for step in range(1, n_protos):
        pl.semaphore_signal(
            barrier, inc=1, device_id={"protos": lax.rem(p + step, n_protos)}, device_id_type=mesh_id
        )
    pl.semaphore_wait(barrier, n_rows + n_protos - 2)

    def where(src, c):
        return full.at[c, pl.ds(pl.multiple_of(src * dim, dim), dim)]

    def given(c):
        return proto_ref.at[:, pl.ds(pl.multiple_of(c * span, span), span)]

    def block_copy(way, src, c, own=False):
        target = {UP: r + 2, DOWN: r - 2, ACROSS: z * 2 + other}[way]
        return pltpu.make_async_remote_copy(
            src_ref=given(c) if own else where(src, c),
            dst_ref=where(src, c),
            send_sem=send.at[way, src, c],
            recv_sem=recv.at[src, c],
            device_id={"rows": target},
            device_id_type=mesh_id,
        )

    def own_copy(c):
        return pltpu.make_async_copy(given(c), where(r, c), own_sem.at[c])

    def send_own(c):
        @pl.when(z < nz - 1)
        def _():
            block_copy(UP, r, c, True).start()

        @pl.when(z > 0)
        def _():
            block_copy(DOWN, r, c, True).start()

        block_copy(ACROSS, r, c, True).start()
        own_copy(c).start()

    def feat_copy(step):
        block = pl.ds(pl.multiple_of(p * fdim, fdim), fdim)
        return pltpu.make_async_remote_copy(
            src_ref=feat_ref,
            dst_ref=feat_full.at[block],
            send_sem=feat_send.at[step],
            recv_sem=feat_recv.at[step],
            device_id={"protos": lax.rem(p + step, n_protos)},
            device_id_type=mesh_id,
        )

    index_in = pltpu.make_async_copy(index_ref, index, in_sem.at[0])
    feat_in = pltpu.make_async_copy(
        feat_ref, feat_full.at[pl.ds(pl.multiple_of(p * fdim, fdim), fdim)], in_sem.at[1]
    )
    for step in range(1, n_protos):
        feat_copy(step).start()
    for c in range(LEAD):
        send_own(c)
    index_in.start()
    feat_in.start()
    onehot[...] = jnp.zeros_like(onehot)
    index_in.wait()
    hits = lax.broadcasted_iota(jnp.int32, (onehot.shape[0], rows), 0) == index[...]
    onehot[:, :rows] = hits.astype(jnp.float32).astype(jnp.bfloat16)
    feat_in.wait()
    for step in range(1, n_protos):
        feat_copy(step).wait()
    picked = jnp.dot(feat_full[...], onehot[...], preferred_element_type=jnp.float32)
    picked = picked.T[:rows]
    chosen[...] = picked.astype(jnp.bfloat16)
    scale = lax.rsqrt(jnp.sum(picked * picked, axis=1, keepdims=True) + EPS)
    feat_scale[...] = jnp.broadcast_to(scale * (1.0 / TEMP), feat_scale.shape)
    acc[...] = jnp.zeros_like(acc)

    def mass_copy(it, c, sender):
        return pltpu.make_async_remote_copy(
            src_ref=parts.at[it, c],
            dst_ref=masses.at[it, sender],
            send_sem=mass_send.at[it, c],
            recv_sem=mass_recv.at[it, sender],
            device_id={"rows": c},
            device_id_type=mesh_id,
        )

    def give_mass(it, c):
        @pl.when(c == r)
        def _():
            masses[it, c] = parts[it, c]

        @pl.when(c != r)
        def _():
            mass_copy(it, c, r).start()

    def make_weights(c):
        for t in range(span // tile):
            columns = pl.ds(pl.multiple_of(c * span + t * tile, tile), tile)
            within = pl.ds(pl.multiple_of(lax.rem(c, SPLIT) * span + t * tile, tile), tile)
            block = full[c, :, t * tile:(t + 1) * tile]
            wide = block.astype(jnp.float32)
            proto_scale = lax.rsqrt(jnp.sum(wide * wide, axis=0, keepdims=True) + EPS)
            raw = jnp.dot(chosen[...], block, preferred_element_type=jnp.float32)
            value = jnp.exp(raw * feat_scale[:, :1] * proto_scale)
            weights[:, columns] = value
            parts[0, c // SPLIT, :, within] = jnp.sum(value, axis=0, keepdims=True)

    def early(c):
        return c == 4

    def line(c, d):
        for way, ahead, more, there in (
            (DOWN, z + d, z > 0, z + d < nz),
            (UP, z - d, z < nz - 1, z - d >= 0),
        ):
            src = ahead * 2 + y

            @pl.when(there)
            def _():
                block_copy(ACROSS, src, c).wait_recv()

                @pl.when(more)
                def _():
                    block_copy(way, src, c).start()

                @pl.when(jnp.logical_not(early(c)))
                def _():
                    block_copy(ACROSS, src, c).start()

    def far_line(c, d):
        for way, ahead, more, there in (
            (DOWN, z + d, z > 0, z + d < nz),
            (UP, z - d, z < nz - 1, z - d >= 0),
        ):
            src = ahead * 2 + other

            @pl.when(there)
            def _():
                block_copy(ACROSS, src, c).wait_recv()

                @pl.when(jnp.logical_and(more, early(c)))
                def _():
                    block_copy(way, src, c).start()

    def beside(c):
        src = z * 2 + other
        block_copy(ACROSS, src, c).wait_recv()

        @pl.when(jnp.logical_and(z < nz - 1, early(c)))
        def _():
            block_copy(UP, src, c).start()

        @pl.when(jnp.logical_and(z > 0, early(c)))
        def _():
            block_copy(DOWN, src, c).start()

    def step_of(i, carry):
        @pl.when(i + LEAD < chunks)
        def _():
            send_own(i + LEAD)

        @pl.when(i < chunks)
        def _():
            beside(i)

        for d in range(1, nz):
            c = i - (d - 1)

            @pl.when(jnp.logical_and(c >= 0, c < chunks))
            def _():
                line(c, d)

        for d in range(1, nz):
            c = i - d

            @pl.when(jnp.logical_and(jnp.logical_and(c >= 0, c < chunks), early(c)))
            def _():
                far_line(c, d)

        last = i - (nz - 1)

        @pl.when(jnp.logical_and(last >= 0, jnp.logical_not(early(last))))
        def _():
            for d in range(1, nz):
                far_line(last, d)

        @pl.when(last >= 0)
        def _():
            own_copy(last).wait()
            make_weights(last)

            @pl.when(lax.rem(last, SPLIT) == SPLIT - 1)
            def _():
                give_mass(0, last // SPLIT)

        return carry

    lax.fori_loop(0, chunks + nz - 1, step_of, 0)

    def scale_copy(it, c, step):
        return pltpu.make_async_remote_copy(
            src_ref=cs_ref.at[it, c],
            dst_ref=cs_ref.at[it, c],
            send_sem=scale_send.at[it, step],
            recv_sem=scale_recv.at[it, c],
            device_id={"rows": lax.rem(r + step, n_rows)},
            device_id_type=mesh_id,
        )

    def row_copy(it, step):
        return pltpu.make_async_remote_copy(
            src_ref=row_out.at[it],
            dst_ref=row_in.at[it, step],
            send_sem=row_send.at[it, step],
            recv_sem=row_recv.at[it, step],
            device_id={"protos": lax.rem(p + step, n_protos)},
            device_id_type=mesh_id,
        )

    for it in range(ITERS):
        if it > 0:
            row_scale = rs_ref[:rows, :1]

            def col_pass(j, carry):
                c = lax.rem(r + 1 + j, n_rows)
                for t in range(tiles):
                    columns = pl.ds(pl.multiple_of(c * width + t * tile, tile), tile)
                    value = jnp.sum(weights[:, columns] * rs_ref[:rows, :1], axis=0, keepdims=True)
                    parts[it, c, :, t * tile:(t + 1) * tile] = value
                give_mass(it, c)
                return carry

            lax.fori_loop(0, n_rows, col_pass, 0)
        for step in range(1, n_rows):
            mass_copy(it, r, lax.rem(r + step, n_rows)).wait_recv()
        cs_ref[it, r] = 1.0 / (protos_all * jnp.sum(masses[it], axis=0))
        for step in range(1, n_rows):
            scale_copy(it, r, step).start()

        def row_pass(j, total):
            c = lax.rem(r + j, n_rows)

            @pl.when(j > 0)
            def _():
                scale_copy(it, c, 1).wait_recv()

            for t in range(width // 128):
                columns = pl.ds(pl.multiple_of(c * width + t * 128, 128), 128)
                total = total + weights[:, columns] * cs_ref[it, c, :, t * 128:(t + 1) * 128]
            return total

        summed = lax.fori_loop(0, n_rows, row_pass, jnp.zeros((rows, 128), jnp.float32))
        acc[:rows, :] = summed
        row_out[it] = jnp.sum(acc[...].T, axis=0, keepdims=True)
        for step in range(1, n_protos):
            row_copy(it, step).start()
        mass = row_out[it]
        for step in range(1, n_protos):
            row_copy(it, step).wait_recv()
            mass = mass + row_in[it, step]
        turned = jnp.broadcast_to(1.0 / (masked * mass), (128, acc.shape[0])).T
        rs_ref[...] = turned

    for it in range(ITERS):
        for step in range(1, n_rows):
            mass_copy(it, lax.rem(r + step, n_rows), r).wait_send()
            scale_copy(it, r, step).wait_send()
        for step in range(1, n_protos):
            row_copy(it, step).wait_send()

    def drain(c, carry):
        for src_z in range(nz):
            for src_y in range(2):
                src = src_z * 2 + src_y
                on_line = src_y == y
                beside_me = jnp.logical_and(src_y != y, src_z == z)
                moved = jnp.logical_or(on_line, early(c))

                @pl.when(jnp.logical_and(moved, jnp.logical_and(src_z <= z, z < nz - 1)))
                def _():
                    block_copy(UP, src, c).wait_send()

                @pl.when(jnp.logical_and(moved, jnp.logical_and(src_z >= z, z > 0)))
                def _():
                    block_copy(DOWN, src, c).wait_send()

                @pl.when(jnp.logical_and(on_line, jnp.logical_or(src_z == z, jnp.logical_not(early(c)))))
                def _():
                    block_copy(ACROSS, src, c).wait_send()

        return carry

    lax.fori_loop(0, chunks, drain, 0)


def finish(factor, weights, rs_ref, cs_ref, out_ref, buffer, out_sem):
    rows, total = weights.shape
    count, width = cs_ref.shape[0], cs_ref.shape[2]
    slots = buffer.shape[0]

    def out_copy(c):
        columns = pl.ds(pl.multiple_of(c * width, width), width)
        slot = lax.rem(c, slots)
        return pltpu.make_async_copy(buffer.at[slot], out_ref.at[:, columns], out_sem.at[slot])

    def block(c, carry):
        @pl.when(c >= slots)
        def _():
            out_copy(c - slots).wait()

        for t in range(width // 128):
            columns = pl.ds(pl.multiple_of(c * width + t * 128, 128), 128)
            col_scale = cs_ref[c, :, t * 128:(t + 1) * 128]
            value = (factor * rs_ref[:rows, :]) * weights[:, columns] * col_scale
            buffer[lax.rem(c, slots), :, t * 128:(t + 1) * 128] = value.astype(jnp.bfloat16)
        out_copy(c).start()
        return carry

    lax.fori_loop(0, count, block, 0)
    for c in range(max(0, count - slots), count):
        out_copy(c).wait()


def with_kernel(n_rows, n_protos, features, prototypes, masked_index):
    rows = masked_index.shape[0]
    dim, total = prototypes.shape[1], prototypes.shape[0]
    fdim, patches = features.shape[1], features.shape[0]
    width = total // n_rows
    padded = -(-rows // 128) * 128
    masked = float(rows * n_rows)
    protos_all = float(total * n_protos)
    f32, bf16, dma = jnp.float32, jnp.bfloat16, pltpu.SemaphoreType.DMA
    vmem = pl.BlockSpec(memory_space=pltpu.VMEM)
    anywhere = pl.BlockSpec(memory_space=pl.ANY)
    weights, rs, cs = pl.pallas_call(
        functools.partial(kernel, n_rows, n_protos, masked, protos_all),
        out_shape=(
            jax.ShapeDtypeStruct((rows, total), f32),
            jax.ShapeDtypeStruct((padded, 128), f32),
            jax.ShapeDtypeStruct((ITERS, n_rows, 1, width), f32),
        ),
        in_specs=[pl.BlockSpec(memory_space=pltpu.HBM)] * 3,
        out_specs=(vmem, vmem, vmem),
        scratch_shapes=[
            pltpu.VMEM((fdim * n_protos, patches), bf16),
            pltpu.VMEM((1, rows), jnp.int32),
            pltpu.VMEM((patches, padded), bf16),
            pltpu.VMEM((n_rows * SPLIT, dim * n_rows, width // SPLIT), bf16),
            pltpu.VMEM((rows, fdim * n_protos), bf16),
            pltpu.VMEM((rows, 128), f32),
            pltpu.VMEM((padded, 128), f32),
            pltpu.VMEM((ITERS, n_rows, 1, width), f32),
            pltpu.VMEM((ITERS, n_rows, 1, width), f32),
            pltpu.VMEM((ITERS, 1, padded), f32),
            pltpu.VMEM((ITERS, n_protos, 1, padded), f32),
            dma((n_protos,)),
            dma((n_protos,)),
            dma((2,)),
            dma((n_rows * SPLIT,)),
            dma((3, n_rows, n_rows * SPLIT)),
            dma((n_rows, n_rows * SPLIT)),
            dma((ITERS, n_rows)),
            dma((ITERS, n_rows)),
            dma((ITERS, n_rows)),
            dma((ITERS, n_rows)),
            dma((ITERS, n_protos)),
            dma((ITERS, n_protos)),
        ],
        compiler_params=pltpu.CompilerParams(
            collective_id=0, has_side_effects=True, vmem_limit_bytes=20 * 1024 * 1024
        ),
    )(features.T, prototypes.T, masked_index[None, :])
    return pl.pallas_call(
        functools.partial(finish, protos_all * masked),
        out_shape=jax.ShapeDtypeStruct((rows, total), bf16),
        in_specs=[vmem, vmem, vmem],
        out_specs=anywhere,
        scratch_shapes=[pltpu.VMEM((4, rows, width), bf16), dma((4,))],
        compiler_params=pltpu.CompilerParams(vmem_limit_bytes=20 * 1024 * 1024),
    )(weights, rs, cs[ITERS - 1])


def with_collectives(features, prototypes, masked_index):
    total_protos = float(prototypes.shape[0] * lax.axis_size("protos"))
    chosen = jnp.take(features, masked_index, axis=0)
    patches = lax.all_gather(chosen, "protos", axis=1, tiled=True)
    feat_scale = lax.rsqrt(jnp.sum(jnp.square(patches.astype(jnp.float32)), axis=1) + EPS)
    full = lax.all_gather(prototypes, "rows", axis=1, tiled=True)
    proto_sq = jnp.sum(jnp.square(full.astype(jnp.float32)), axis=1)
    raw = lax.dot_general(
        patches, full, (((1,), (1,)), ((), ())), preferred_element_type=jnp.float32
    )
    proto_scale = lax.rsqrt(proto_sq + EPS)
    weights = jnp.exp(raw * feat_scale[:, None] * proto_scale[None, :] / TEMP)
    total_rows = masked_index.shape[0] * lax.axis_size("rows")
    row_scale = jnp.ones((patches.shape[0],), jnp.float32)
    for step in range(ITERS):
        col_part = jnp.dot(row_scale, weights, precision=lax.Precision.HIGHEST)
        col_scale = 1.0 / (total_protos * lax.psum(col_part, "rows"))
        row_part = jnp.dot(weights, col_scale, precision=lax.Precision.HIGHEST)
        row_scale = 1.0 / (total_rows * lax.psum(row_part, "protos"))
    factor = total_protos * float(total_rows)
    return (factor * row_scale[:, None] * weights * col_scale[None, :]).astype(jnp.bfloat16)


def solution(mesh):
    n_rows, n_protos = mesh.shape["rows"], mesh.shape["protos"]
    in_specs = (P("rows", "protos"), P("protos", "rows"), P("rows"))
    out_specs = P("rows", "protos")

    def on_device(features, prototypes, masked_index):
        fits = (
            n_rows % 2 == 0
            and n_rows <= 8
            and prototypes.shape[1] % 16 == 0
            and features.shape[1] % 16 == 0
            and prototypes.shape[0] % (n_rows * SPLIT * 128) == 0
        )
        if fits:
            return with_kernel(n_rows, n_protos, features, prototypes, masked_index)
        return with_collectives(features, prototypes, masked_index)

    return jax.shard_map(
        on_device, mesh=mesh, in_specs=in_specs, out_specs=out_specs, check_vma=False
    )
```

profile of v0, /device:TPU:4, one launch (start us, length us, event | category | flops | bytes accessed | tf_op | source)
XLA Modules:
  0.0 134.0 jit_solution(6021169992642667616)
XLA Ops:
  0.0 0.0 copy-start
  0.0 1.2 copy-done
  1.2 0.0 copy-start.1
  1.2 0.8 copy-done.1
  2.0 0.0 copy-start.2
  2.0 0.7 copy-done.2
  2.7 128.2 %shard_map.37 = (f32[192,16384]{1,0:T(8,128)S(1)}, f32[256,128]{1,0:T(8,128)S(1)}, f32[3,8,1,2048]{3,2,1,0:T(1,128)S(1)}) custom-call(bf16[64,384]{1,0:T(8,128)(2,1)S(1)} %bitcast.6, bf16[32,16384]{1,0:T(8,128)(2,1)S(1)} %bitcast.5, s32[1,192]{1,0:T(1,128)S(1)} %bitcast.7), custom_call_target="tpu_custom_call" | custom-call | tf_op jit(solution)/shard_map/pallas_call | solution.py:377
  130.9 3.1 %shard_map.38 = bf16[192,16384]{1,0:T(8,128)(2,1)} custom-call(f32[192,16384]{1,0:T(8,128)S(1)} %get-tuple-element.8.weights, f32[256,128]{1,0:T(8,128)S(1)} %get-tuple-element.9.rs_ref, f32[8,1,2048]{2,1,0:T(1,128)S(1)} %slice_bitcast_fusion.cs_ref), custom_call_target="tpu_custom_call" | custom-call | tf_op jit(solution)/shard_map/pallas_call | solution.py:415
  (1 shorter events, 0.0 us)
Async XLA Ops:
  0.0 1.2 copy-start
  1.2 0.8 copy-start.1
  2.0 0.7 copy-start.2
where the time goes:
time: 136 us; the launch traced here: 134 us
  Pallas kernels  131 us (96%)
  local copies, waits for them, and re-layouts  2.71 us (2%)
    pallas_call x1, Pallas kernels, with_kernel(): pl.pallas_call(functools.partial(kernel, n_rows, n_protos, masked, protos...  128 us
    pallas_call x1, Pallas kernels, with_kernel(): pl.pallas_call(functools.partial(finish, protos_all * masked), out_shape=...  3.08 us

commit v1 on v0

v1 whole, which is shorter than its diff:
```python
import functools

import jax
import jax.numpy as jnp
from jax import lax
from jax.experimental import pallas as pl
from jax.experimental.pallas import tpu as pltpu
from jax.sharding import PartitionSpec as P

ITERS = 3


TEMP = 0.07
EPS = 1e-06
LOG2E = 1.4426950408889634
UP, DOWN, ACROSS = 0, 1, 2
LEAD = 6
SPLIT = 2
EARLY = (5, 10)
LAG = 4
BLOCK = 128


def kernel(
    n_rows, n_protos, masked, protos_all,
    feat_ref, proto_ref, index_ref, out_ref,
    feat_in, index, onehot, picks, patches, pair, chosen, lane_scale, feat_scale, full, weights,
    acc, row_out, row_in, mass_out, mass_in, row_scale, out_scale, scales,
    in_sem, own_sem, pick_send, pick_recv, patch_send, patch_recv, send, recv, direct_send,
    row_send, row_recv, mass_send, mass_recv, scale_send, scale_recv,
):
    r, p = lax.axis_index("rows"), lax.axis_index("protos")
    z, y = r // 2, lax.rem(r, 2)
    nz = n_rows // 2
    other = z * 2 + 1 - y
    dim, total = proto_ref.shape
    width = total // n_rows
    chunks = n_rows * SPLIT
    span = total // chunks
    rows = index_ref.shape[1]
    fdim = feat_ref.shape[0]
    lanes = rows * n_rows
    odd = y == 1
    both = jnp.logical_and
    no = jnp.logical_not
    mesh_id = pl.DeviceIdType.MESH

    def where(src, c):
        return full.at[c, pl.ds(pl.multiple_of(src * dim, dim), dim)]

    def own_copy(c):
        return pltpu.make_async_copy(
            proto_ref.at[:, pl.ds(pl.multiple_of(c * span, span), span)], where(r, c), own_sem.at[c]
        )

    def early(c):
        hit = c == EARLY[0]
        for e in EARLY[1:]:
            hit = jnp.logical_or(hit, c == e)
        return hit

    def owner(c):
        return c // SPLIT

    def plane(c):
        return c // (2 * SPLIT)

    def remote(src, dst, send_sem, recv_sem, **device):
        return pltpu.make_async_remote_copy(
            src_ref=src, dst_ref=dst, send_sem=send_sem, recv_sem=recv_sem,
            device_id=device, device_id_type=mesh_id,
        )

    def block_copy(way, src, c):
        target = {UP: r + 2, DOWN: r - 2, ACROSS: other}[way]
        return remote(where(src, c), where(src, c), send.at[way, src, c], recv.at[src, c], rows=target)

    def when(condition, action):
        @pl.when(condition)
        def _():
            action()

    def each(count, body):
        def step(i, carry):
            body(i)
            return carry

        lax.fori_loop(0, count, step, 0)

    def goes_up(c, on_line):
        return both(z < nz - 1, plane(c) != z + 1 if on_line else owner(c) != r + 2)

    def goes_down(c, on_line):
        return both(z > 0, plane(c) != z - 1 if on_line else owner(c) != r - 2)

    def direct_copy(step, c):
        target = lax.rem(r + 2 * step, n_rows)
        chunk = target // 2 * (2 * SPLIT) + c
        return remote(
            where(r, chunk), where(r, chunk), direct_send.at[step, c], recv.at[r, chunk], rows=target
        )

    def pick_copy(step):
        return remote(
            picks.at[r], picks.at[r], pick_send.at[step], pick_recv.at[r], rows=lax.rem(r + step, n_rows)
        )

    def pick_from(src):
        return remote(picks.at[src], picks.at[src], pick_send.at[0], pick_recv.at[src], rows=other)

    def patch_copy(step, src):
        part = patches.at[pl.ds(pl.multiple_of(src * fdim, fdim), fdim)]
        return remote(
            part, part, patch_send.at[step], patch_recv.at[src], protos=lax.rem(p + step, n_protos)
        )

    def row_copy(it, step):
        return remote(
            row_out.at[it], row_in.at[it, step], row_send.at[it, step], row_recv.at[it, step],
            protos=lax.rem(p + step, n_protos),
        )

    def mass_copy(it, step):
        return remote(
            mass_out.at[it], mass_in.at[it, step], mass_send.at[it, step], mass_recv.at[it, step],
            rows=lax.rem(r + step, n_rows),
        )

    def scale_copy(step, src):
        return remote(
            scales.at[src], scales.at[src], scale_send.at[step], scale_recv.at[src],
            rows=lax.rem(r + step, n_rows),
        )

    feat_load = pltpu.make_async_copy(feat_ref, feat_in, in_sem.at[0])
    index_load = pltpu.make_async_copy(index_ref, index, in_sem.at[1])
    feat_load.start()
    index_load.start()
    each(chunks, lambda c: own_copy(c).start())

    barrier = pltpu.get_barrier_semaphore()
    for step in range(1, n_rows):
        pl.semaphore_signal(
            barrier, inc=1, device_id={"rows": lax.rem(r + step, n_rows)}, device_id_type=mesh_id
        )
    for step in range(1, n_protos):
        pl.semaphore_signal(
            barrier, inc=1, device_id={"protos": lax.rem(p + step, n_protos)}, device_id_type=mesh_id
        )

    onehot[...] = jnp.zeros_like(onehot)
    index_load.wait()
    hits = lax.broadcasted_iota(jnp.int32, (onehot.shape[0], rows), 0) == index[...]
    onehot[:, :rows] = hits.astype(jnp.float32).astype(jnp.bfloat16)
    feat_load.wait()
    picked = jnp.dot(feat_in[...], onehot[...], preferred_element_type=jnp.float32)
    picked = jnp.where(odd, pltpu.roll(picked, 2 * BLOCK - rows, 1), picked)
    picks[r] = picked.astype(jnp.bfloat16)
    acc[...] = jnp.zeros_like(acc)
    each(chunks, lambda c: own_copy(c).wait())

    pl.semaphore_wait(barrier, n_rows + n_protos - 2)

    for step in range(1, n_rows):
        pick_copy(step).start()

    def begin(c):
        when(both(owner(c) == other, c >= 0), lambda: block_copy(ACROSS, r, c).start())

    each(chunks, begin)
    for step in range(1, nz):
        for c in range(2 * SPLIT):
            direct_copy(step, c).start()

    def send_own(c):
        when(goes_up(c, True), lambda: block_copy(UP, r, c).start())
        when(goes_down(c, True), lambda: block_copy(DOWN, r, c).start())
        when(owner(c) != other, lambda: block_copy(ACROSS, r, c).start())

    each(LEAD, send_own)

    for step in range(1, n_rows):
        pick_from(lax.rem(r + step, n_rows)).wait_recv()
    mine = pl.ds(pl.multiple_of(p * fdim, fdim), fdim)
    for j in range(nz):
        at = 3 * BLOCK * j
        patches[mine, at:at + BLOCK] = picks[2 * j, :, :BLOCK]
        patches[mine, at + BLOCK:at + 2 * BLOCK] = (
            picks[2 * j, :, BLOCK:].astype(jnp.float32) + picks[2 * j + 1, :, :BLOCK].astype(jnp.float32)
        ).astype(jnp.bfloat16)
        patches[mine, at + 2 * BLOCK:at + 3 * BLOCK] = picks[2 * j + 1, :, BLOCK:]
    for step in range(1, n_protos):
        patch_copy(step, p).start()

    def relay(step):
        src = lax.rem(r + 2 * step, n_rows)
        for j in range(SPLIT):
            block_copy(ACROSS, src, other * SPLIT + j).wait_recv()
            block_copy(ACROSS, src, other * SPLIT + j).start()
        for j in range(SPLIT):
            block_copy(ACROSS, src, r * SPLIT + j).wait_recv()

    for step in range(1, nz):
        relay(step)

    for step in range(1, n_protos):
        patch_copy(step, lax.rem(p + step, n_protos)).wait_recv()
    pair[...] = patches[:, pl.ds(pl.multiple_of(z * (2 * rows), 2 * rows), 2 * rows)].T
    chosen[...] = pair[pl.ds(pl.multiple_of(y * rows, rows), rows), :]
    wide = chosen[...].astype(jnp.float32)
    scale = lax.rsqrt(jnp.sum(wide * wide, axis=1, keepdims=True) + EPS)
    feat_scale[...] = jnp.broadcast_to(scale * (LOG2E / TEMP), feat_scale.shape)
    for t in range(lanes // BLOCK):
        wide = patches[:, t * BLOCK:(t + 1) * BLOCK].astype(jnp.float32)
        scale = lax.rsqrt(jnp.sum(wide * wide, axis=0, keepdims=True) + EPS)
        lane_scale[:, t * BLOCK:(t + 1) * BLOCK] = scale * (LOG2E / TEMP)
    for step in range(nz):
        src = lax.rem(other + 2 * step, n_rows)
        for j in range(SPLIT):
            block_copy(ACROSS, src, r * SPLIT + j).wait_recv()

    def turned(column):
        return jnp.broadcast_to(column, (BLOCK, BLOCK)).T[:1]

    def add_rows(value, col_mass, tile):
        col_scale = 1.0 / (protos_all * col_mass)
        scaled = (value * col_scale).reshape(BLOCK // 8, 8, lanes)
        acc[...] += jnp.sum(scaled, axis=0)
        return col_scale

    def make_weights(half):
        def body(i):
            tile = half * (width // BLOCK // 2) + i
            per = span // BLOCK
            within = pl.ds(pl.multiple_of(lax.rem(tile, per) * BLOCK, BLOCK), BLOCK)
            block = full[r * SPLIT + tile // per, :, within].T
            wide = block.astype(jnp.float32)
            proto_scale = lax.rsqrt(jnp.sum(wide * wide, axis=1, keepdims=True) + EPS)
            raw = jnp.dot(block, patches[...], preferred_element_type=jnp.float32)
            value = jnp.exp2(raw * lane_scale[...] * proto_scale)
            weights[pl.ds(pl.multiple_of(tile * BLOCK, BLOCK), BLOCK)] = value
            add_rows(value, jnp.sum(value, axis=1, keepdims=True), tile)
            scales[r, 1, :, pl.ds(pl.multiple_of(tile * BLOCK, BLOCK), BLOCK)] = turned(proto_scale)

        each(width // BLOCK // 2, body)

    def one_pass(it):
        def body(tile):
            at = pl.ds(pl.multiple_of(tile * BLOCK, BLOCK), BLOCK)
            value = weights[at]
            col_mass = jnp.sum(value * row_scale[...], axis=1, keepdims=True)
            col_scale = add_rows(value, col_mass, tile)
            if it == ITERS - 1:
                scales[r, 0, :, at] = turned(col_scale)

        each(width // BLOCK, body)

    def give_rows(it):
        row_out[it] = jnp.sum(acc[...], axis=0, keepdims=True)
        acc[...] = jnp.zeros_like(acc)
        for step in range(1, n_protos):
            row_copy(it, step).start()

    def give_mass(it):
        mass = row_out[it]
        for step in range(1, n_protos):
            row_copy(it, step).wait_recv()
            mass = mass + row_in[it, step]
        mass_out[it] = mass
        for step in range(1, n_rows):
            mass_copy(it, step).start()

    def take_mass(it):
        mass = mass_out[it]
        for step in range(1, n_rows):
            mass_copy(it, step).wait_recv()
            mass = mass + mass_in[it, step]
        row_scale[...] = 1.0 / (masked * mass)

    def next_pass(it):
        take_mass(it - 1)
        one_pass(it)
        if it == ITERS - 1:
            for step in range(1, n_rows):
                scale_copy(step, r).start()
        give_rows(it)

    def settle():
        take_mass(ITERS - 1)
        at = lax.broadcasted_iota(jnp.int32, (rows, lanes), 1)
        row = lax.broadcasted_iota(jnp.int32, (rows, lanes), 0) + r * rows
        found = jnp.where(at == row, jnp.broadcast_to(row_scale[...], (rows, lanes)), 0.0)
        found = jnp.sum(found, axis=1, keepdims=True) * (protos_all * masked)
        out_scale[...] = jnp.broadcast_to(found, out_scale.shape)
        for step in range(1, n_rows):
            scale_copy(step, lax.rem(r + step, n_rows)).wait_recv()

    def make_output(c):
        tile = min(512, span)
        for t in range(span // tile):
            block = full[c, :, t * tile:(t + 1) * tile]
            raw = jnp.dot(chosen[...], block, preferred_element_type=jnp.float32)
            at = pl.ds(pl.multiple_of(lax.rem(c, SPLIT) * span + t * tile, tile), tile)
            value = jnp.exp2(raw * feat_scale[:, :1] * scales[owner(c), 1, :, at])
            value = out_scale[:, :1] * value * scales[owner(c), 0, :, at]
            out_ref[c, :, t * tile:(t + 1) * tile] = value.astype(jnp.bfloat16)

    stages = {
        0: lambda: make_weights(0),
        1: lambda: (make_weights(1), give_rows(0)),
        2: lambda: give_mass(0),
        4: lambda: next_pass(1),
        5: lambda: give_mass(1),
        7: lambda: next_pass(2),
        8: lambda: give_mass(2),
        10: settle,
    }
    first = 11
    pace = 4

    def beside(c):
        src = other
        when(owner(c) != r, lambda: block_copy(ACROSS, src, c).wait_recv())
        when(both(early(c), goes_up(c, False)), lambda: block_copy(UP, src, c).start())
        when(both(early(c), goes_down(c, False)), lambda: block_copy(DOWN, src, c).start())

    def ways(d):
        return (
            (DOWN, z + d, goes_down, z + d < nz),
            (UP, z - d, goes_up, z - d >= 0),
        )

    def line(c, d):
        for way, ahead, more, there in ways(d):
            src = ahead * 2 + y

            @pl.when(there)
            def _():
                when(plane(c) != z, lambda: block_copy(ACROSS, src, c).wait_recv())
                when(more(c, True), lambda: block_copy(way, src, c).start())
                when(
                    both(no(early(c)), owner(c) != other), lambda: block_copy(ACROSS, src, c).start()
                )

    def far_line(c, d):
        for way, ahead, more, there in ways(d):
            src = ahead * 2 + 1 - y

            @pl.when(there)
            def _():
                when(owner(c) != r, lambda: block_copy(ACROSS, src, c).wait_recv())
                when(both(early(c), more(c, False)), lambda: block_copy(way, src, c).start())

    def drain(c):
        for src_z in range(nz):
            for src_y in range(2):
                src = src_z * 2 + src_y
                on_line = src_y == y
                up = jnp.where(on_line, goes_up(c, True), both(early(c), goes_up(c, False)))
                down = jnp.where(on_line, goes_down(c, True), both(early(c), goes_down(c, False)))
                kept = both(src_z != z, both(early(c), owner(c) != other))
                when(both(up, src_z <= z), lambda: block_copy(UP, src, c).wait_send())
                when(both(down, src_z >= z), lambda: block_copy(DOWN, src, c).wait_send())
                when(both(on_line, no(kept)), lambda: block_copy(ACROSS, src, c).wait_send())

    def done_by(i):
        return jnp.clip(jnp.minimum((i - first + 1) * pace, i - nz + 2), 0, chunks)

    def step_of(i, carry):
        when(i + LEAD < chunks, lambda: send_own(i + LEAD))
        when(i < chunks, lambda: beside(i))
        for d in range(1, nz):
            c = i - (d - 1)
            when(both(c >= 0, c < chunks), lambda: line(c, d))
        for d in range(1, nz):
            c = i - d
            when(both(both(c >= 0, c < chunks), early(c)), lambda: far_line(c, d))
        last = i - (nz - 1)

        @pl.when(both(last >= 0, no(early(last))))
        def _():
            for d in range(1, nz):
                far_line(last, d)

        for at, stage in stages.items():
            when(i == at, stage)

        def output(c, carry):
            make_output(c)
            return carry

        lax.fori_loop(done_by(i - 1), done_by(i), output, 0)
        when(last >= LAG, lambda: drain(last - LAG))
        return carry

    steps = chunks + nz - 1
    lax.fori_loop(0, steps, step_of, 0)

    for step in range(1, n_rows):
        pick_copy(step).wait_send()
        scale_copy(step, r).wait_send()
    for step in range(1, nz):
        for c in range(2 * SPLIT):
            direct_copy(step, c).wait_send()
    for step in range(1, n_protos):
        patch_copy(step, p).wait_send()
    for it in range(ITERS):
        for step in range(1, n_rows):
            mass_copy(it, step).wait_send()
        for step in range(1, n_protos):
            row_copy(it, step).wait_send()

    def rest(i, carry):
        drain(i)
        return carry

    lax.fori_loop(chunks - LAG, chunks, rest, 0)


def finish(blocks_ref, out_ref, out_sem):
    count, rows, span = blocks_ref.shape
    copies = [
        pltpu.make_async_copy(
            blocks_ref.at[c], out_ref.at[:, c * span:(c + 1) * span], out_sem.at[c]
        )
        for c in range(count)
    ]
    for copy in copies:
        copy.start()
    for copy in copies:
        copy.wait()


def with_kernel(n_rows, n_protos, features, prototypes, masked_index):
    rows = masked_index.shape[0]
    dim, total = prototypes.shape[1], prototypes.shape[0]
    fdim, patches = features.shape[1], features.shape[0]
    width = total // n_rows
    chunks = n_rows * SPLIT
    span = total // chunks
    lanes = rows * n_rows
    depth = fdim * n_protos
    masked = float(lanes)
    protos_all = float(total * n_protos)
    f32, bf16, dma = jnp.float32, jnp.bfloat16, pltpu.SemaphoreType.DMA
    vmem = pl.BlockSpec(memory_space=pltpu.VMEM)
    anywhere = pl.BlockSpec(memory_space=pl.ANY)
    blocks = pl.pallas_call(
        functools.partial(kernel, n_rows, n_protos, masked, protos_all),
        out_shape=jax.ShapeDtypeStruct((chunks, rows, span), bf16),
        in_specs=[pl.BlockSpec(memory_space=pltpu.HBM)] * 3,
        out_specs=vmem,
        scratch_shapes=[
            pltpu.VMEM((fdim, patches), bf16),
            pltpu.VMEM((1, rows), jnp.int32),
            pltpu.VMEM((patches, 2 * BLOCK), bf16),
            pltpu.VMEM((n_rows, fdim, 2 * BLOCK), bf16),
            pltpu.VMEM((depth, lanes), bf16),
            pltpu.VMEM((2 * rows, depth), bf16),
            pltpu.VMEM((rows, depth), bf16),
            pltpu.VMEM((1, lanes), f32),
            pltpu.VMEM((rows, BLOCK), f32),
            pltpu.VMEM((chunks, dim * n_rows, span), bf16),
            pltpu.VMEM((width, lanes), f32),
            pltpu.VMEM((8, lanes), f32),
            pltpu.VMEM((ITERS, 1, lanes), f32),
            pltpu.VMEM((ITERS, n_protos, 1, lanes), f32),
            pltpu.VMEM((ITERS, 1, lanes), f32),
            pltpu.VMEM((ITERS, n_rows, 1, lanes), f32),
            pltpu.VMEM((1, lanes), f32),
            pltpu.VMEM((rows, BLOCK), f32),
            pltpu.VMEM((n_rows, 2, 1, width), f32),
            dma((2,)),
            dma((chunks,)),
            dma((n_rows,)),
            dma((n_rows,)),
            dma((n_protos,)),
            dma((n_protos,)),
            dma((3, n_rows, chunks)),
            dma((n_rows, chunks)),
            dma((n_rows // 2, 2 * SPLIT)),
            dma((ITERS, n_protos)),
            dma((ITERS, n_protos)),
            dma((ITERS, n_rows)),
            dma((ITERS, n_rows)),
            dma((n_rows,)),
            dma((n_rows,)),
        ],
        compiler_params=pltpu.CompilerParams(
            collective_id=0, has_side_effects=True, vmem_limit_bytes=56 * 1024 * 1024
        ),
    )(features.T, prototypes.T, masked_index[None, :])
    return pl.pallas_call(
        finish,
        out_shape=jax.ShapeDtypeStruct((rows, total), bf16),
        in_specs=[vmem],
        out_specs=anywhere,
        scratch_shapes=[dma((chunks,))],
        compiler_params=pltpu.CompilerParams(vmem_limit_bytes=4 * 1024 * 1024),
    )(blocks)


def with_collectives(features, prototypes, masked_index):
    total_protos = float(prototypes.shape[0] * lax.axis_size("protos"))
    chosen = jnp.take(features, masked_index, axis=0)
    patches = lax.all_gather(chosen, "protos", axis=1, tiled=True)
    feat_scale = lax.rsqrt(jnp.sum(jnp.square(patches.astype(jnp.float32)), axis=1) + EPS)
    full = lax.all_gather(prototypes, "rows", axis=1, tiled=True)
    proto_sq = jnp.sum(jnp.square(full.astype(jnp.float32)), axis=1)
    raw = lax.dot_general(
        patches, full, (((1,), (1,)), ((), ())), preferred_element_type=jnp.float32
    )
    proto_scale = lax.rsqrt(proto_sq + EPS)
    weights = jnp.exp(raw * feat_scale[:, None] * proto_scale[None, :] / TEMP)
    total_rows = masked_index.shape[0] * lax.axis_size("rows")
    row_scale = jnp.ones((patches.shape[0],), jnp.float32)
    for step in range(ITERS):
        col_part = jnp.dot(row_scale, weights, precision=lax.Precision.HIGHEST)
        col_scale = 1.0 / (total_protos * lax.psum(col_part, "rows"))
        row_part = jnp.dot(weights, col_scale, precision=lax.Precision.HIGHEST)
        row_scale = 1.0 / (total_rows * lax.psum(row_part, "protos"))
    factor = total_protos * float(total_rows)
    return (factor * row_scale[:, None] * weights * col_scale[None, :]).astype(jnp.bfloat16)


def solution(mesh):
    n_rows, n_protos = mesh.shape["rows"], mesh.shape["protos"]
    in_specs = (P("rows", "protos"), P("protos", "rows"), P("rows"))
    out_specs = P("rows", "protos")

    def on_device(features, prototypes, masked_index):
        fits = (
            n_rows % 2 == 0
            and n_rows == 8
            and n_protos > 1
            and prototypes.shape[1] % 16 == 0
            and features.shape[1] % 16 == 0
            and features.shape[1] * n_protos == prototypes.shape[1] * n_rows
            and 2 * masked_index.shape[0] == 3 * BLOCK
            and prototypes.shape[0] % (n_rows * SPLIT * 512) == 0
        )
        if fits:
            return with_kernel(n_rows, n_protos, features, prototypes, masked_index)
        return with_collectives(features, prototypes, masked_index)

    return jax.shard_map(
        on_device, mesh=mesh, in_specs=in_specs, out_specs=out_specs, check_vma=False
    )
```

time: 136 us -> 139 us (1.022)
  Pallas kernels: 131 us -> 135 us
    pallas_call x1, Pallas kernels: 128 us -> 132 us  [with_kernel(): pl.pallas_call(functools.partial(kernel, n_rows, n_protos, masked, protos...]
where the time goes in v1:
time: 139 us; the launch traced here: 138 us
  Pallas kernels  135 us (97%)
  local copies, waits for them, and re-layouts  2.78 us (2%)
    pallas_call x1, Pallas kernels, with_kernel(): pl.pallas_call(functools.partial(kernel, n_rows, n_protos, masked, protos...  132 us

profile of v1, /device:TPU:4, one launch (start us, length us, event | category | flops | bytes accessed | tf_op | source)
XLA Modules:
  0.0 137.5 jit_solution(10248171707767891659)
XLA Ops:
  0.0 132.0 %shard_map.37.blocks_ref = bf16[16,192,1024]{2,1,0:T(8,128)(2,1)} custom-call(bf16[64,384]{1,0:T(8,128)(2,1)} %bitcast.4, bf16[32,16384]{1,0:T(8,128)(2,1)} %bitcast.3, s32[1,192]{1,0:T(1,128)} %bitcast.5), custom_call_target="tpu_custom_call" | custom-call | tf_op jit(solution)/shard_map/pallas_call | solution.py:448
  132.0 0.0 copy-start
  132.0 2.8 %copy-done = bf16[16,192,1024]{2,1,0:T(8,128)(2,1)S(1)} copy-done((bf16[16,192,1024]{2,1,0:T(8,128)(2,1)S(1)}, bf16[16,192,1024]{2,1,0:T(8,128)(2,1)}, u32[]{:S(2)}) %copy-start) | copy-done | bytes 6291480
  134.8 2.8 %shard_map.38 = bf16[192,16384]{1,0:T(8,128)(2,1)} custom-call(bf16[16,192,1024]{2,1,0:T(8,128)(2,1)S(1)} %copy-done), custom_call_target="tpu_custom_call" | custom-call | tf_op jit(solution)/shard_map/pallas_call | solution.py:493
Async XLA Ops:
  132.0 2.8 %copy-start = (bf16[16,192,1024]{2,1,0:T(8,128)(2,1)S(1)}, bf16[16,192,1024]{2,1,0:T(8,128)(2,1)}, u32[]{:S(2)}) copy-start(bf16[16,192,1024]{2,1,0:T(8,128)(2,1)} %shard_map.37.blocks_ref) | copy-start | bytes 18874372

commit v2 on v1

--- a/solution.py
+++ b/solution.py
@@ -14,10 +14,13 @@
 EPS = 1e-06
 LOG2E = 1.4426950408889634
 UP, DOWN, ACROSS = 0, 1, 2
-LEAD = 6
-SPLIT = 2
-EARLY = (5, 10)
-LAG = 4
+LEAD_Z = (8, 3, 6, 0)
+LEAD_Y = 8
+SPLIT = 1
+EARLY = (4,)
+EARLY_AT = 3
+LAG = 2
+STATS_AT = 0
 BLOCK = 128
 
 
@@ -168,16 +171,37 @@
         when(both(owner(c) == other, c >= 0), lambda: block_copy(ACROSS, r, c).start())
 
     each(chunks, begin)
-    for step in range(1, nz):
-        for c in range(2 * SPLIT):
-            direct_copy(step, c).start()
-
-    def send_own(c):
-        when(goes_up(c, True), lambda: block_copy(UP, r, c).start())
-        when(goes_down(c, True), lambda: block_copy(DOWN, r, c).start())
-        when(owner(c) != other, lambda: block_copy(ACROSS, r, c).start())
-
-    each(LEAD, send_own)
+    for apart in range(1, nz):
+        for side in (1, -1):
+            there = both(z + side * apart >= 0, z + side * apart < nz)
+            for c in range(2 * SPLIT):
+                when(there, lambda: direct_copy(lax.rem(nz + side * apart, nz), c).start())
+
+    def order(way, k):
+        if way == ACROSS:
+            swapped = jnp.where(both(k >= EARLY_AT, k <= EARLY_AT + 1), 2 * EARLY_AT + 1 - k, k)
+            return jnp.where(z < nz // 2, chunks - 1 - k, swapped)
+        return k if way == UP else chunks - 1 - k
+
+    def lead(way):
+        behind = z if way == UP else nz - 1 - z
+        count = LEAD_Z[nz - 1]
+        for at in range(nz - 1):
+            count = jnp.where(behind == at, LEAD_Z[at], count)
+        return count
+
+    def own_line(way, k):
+        c = order(way, k)
+        more = (goes_up if way == UP else goes_down)(c, True)
+        when(both(k < chunks, more), lambda: block_copy(way, r, c).start())
+
+    def own_across(k):
+        c = order(ACROSS, k)
+        when(both(k < chunks, owner(c) != other), lambda: block_copy(ACROSS, r, c).start())
+
+    for way in (DOWN, UP):
+        each(lead(way), functools.partial(own_line, way))
+    each(LEAD_Y, own_across)
 
     for step in range(1, n_rows):
         pick_from(lax.rem(r + step, n_rows)).wait_recv()
@@ -192,32 +216,43 @@
     for step in range(1, n_protos):
         patch_copy(step, p).start()
 
-    def relay(step):
-        src = lax.rem(r + 2 * step, n_rows)
-        for j in range(SPLIT):
-            block_copy(ACROSS, src, other * SPLIT + j).wait_recv()
-            block_copy(ACROSS, src, other * SPLIT + j).start()
-        for j in range(SPLIT):
-            block_copy(ACROSS, src, r * SPLIT + j).wait_recv()
-
-    for step in range(1, nz):
-        relay(step)
-
-    for step in range(1, n_protos):
-        patch_copy(step, lax.rem(p + step, n_protos)).wait_recv()
-    pair[...] = patches[:, pl.ds(pl.multiple_of(z * (2 * rows), 2 * rows), 2 * rows)].T
-    chosen[...] = pair[pl.ds(pl.multiple_of(y * rows, rows), rows), :]
-    wide = chosen[...].astype(jnp.float32)
-    scale = lax.rsqrt(jnp.sum(wide * wide, axis=1, keepdims=True) + EPS)
-    feat_scale[...] = jnp.broadcast_to(scale * (LOG2E / TEMP), feat_scale.shape)
-    for t in range(lanes // BLOCK):
-        wide = patches[:, t * BLOCK:(t + 1) * BLOCK].astype(jnp.float32)
-        scale = lax.rsqrt(jnp.sum(wide * wide, axis=0, keepdims=True) + EPS)
-        lane_scale[:, t * BLOCK:(t + 1) * BLOCK] = scale * (LOG2E / TEMP)
-    for step in range(nz):
-        src = lax.rem(other + 2 * step, n_rows)
-        for j in range(SPLIT):
-            block_copy(ACROSS, src, r * SPLIT + j).wait_recv()
+    def relay():
+        for apart in range(1, nz):
+            for side in (1, -1):
+                ahead = z + side * apart
+                src = ahead * 2 + y
+
+                @pl.when(both(ahead >= 0, ahead < nz))
+                def _():
+                    for j in range(SPLIT):
+                        block_copy(ACROSS, src, other * SPLIT + j).wait_recv()
+                        block_copy(ACROSS, src, other * SPLIT + j).start()
+                    for j in range(SPLIT):
+                        block_copy(ACROSS, src, r * SPLIT + j).wait_recv()
+
+    def take_patches():
+        for step in range(1, n_protos):
+            patch_copy(step, lax.rem(p + step, n_protos)).wait_recv()
+        pair[...] = patches[:, pl.ds(pl.multiple_of(z * (2 * rows), 2 * rows), 2 * rows)].T
+        chosen[...] = pair[pl.ds(pl.multiple_of(y * rows, rows), rows), :]
+        wide = chosen[...].astype(jnp.float32)
+        scale = lax.rsqrt(jnp.sum(wide * wide, axis=1, keepdims=True) + EPS)
+        feat_scale[...] = jnp.broadcast_to(scale * (LOG2E / TEMP), feat_scale.shape)
+        for t in range(lanes // BLOCK):
+            wide = patches[:, t * BLOCK:(t + 1) * BLOCK].astype(jnp.float32)
+            scale = lax.rsqrt(jnp.sum(wide * wide, axis=0, keepdims=True) + EPS)
+            lane_scale[:, t * BLOCK:(t + 1) * BLOCK] = scale * (LOG2E / TEMP)
+
+    def take_own():
+        for step in range(nz):
+            src = lax.rem(other + 2 * step, n_rows)
+            apart = jnp.abs(src // 2 - z)
+            for j in range(SPLIT):
+                c = r * SPLIT + j
+                k = jnp.where(src // 2 > z, order(DOWN, c), c)
+                at = jnp.where(early(c), EARLY_AT + apart, k + nz - 1)
+                at = jnp.where(apart == 0, order(ACROSS, c), at)
+                when(at > STATS_AT, lambda: block_copy(ACROSS, src, c).wait_recv())
 
     def turned(column):
         return jnp.broadcast_to(column, (BLOCK, BLOCK)).T[:1]
@@ -306,21 +341,30 @@
             out_ref[c, :, t * tile:(t + 1) * tile] = value.astype(jnp.bfloat16)
 
     stages = {
-        0: lambda: make_weights(0),
-        1: lambda: (make_weights(1), give_rows(0)),
-        2: lambda: give_mass(0),
-        4: lambda: next_pass(1),
-        5: lambda: give_mass(1),
-        7: lambda: next_pass(2),
-        8: lambda: give_mass(2),
-        10: settle,
+        (0, 2): take_patches,
+        (STATS_AT, 3): take_own,
+        (1, 0): lambda: make_weights(0),
+        (1, 2): lambda: (make_weights(1), give_rows(0)),
+        (1, 3): lambda: give_mass(0),
+        (2, 3): lambda: next_pass(1),
+        (3, 1): lambda: give_mass(1),
+        (4, 2): lambda: next_pass(2),
+        (4, 3): lambda: give_mass(2),
+        (6, 1): settle,
     }
-    first = 11
+    first = 6
+
+    def hooks(i, place):
+        for (at, position), stage in stages.items():
+            if position == place:
+                when(i == at, stage)
+
     pace = 4
 
-    def beside(c):
+    def beside(i):
+        c = order(ACROSS, i)
         src = other
-        when(owner(c) != r, lambda: block_copy(ACROSS, src, c).wait_recv())
+        when(jnp.logical_or(owner(c) != r, i <= STATS_AT), lambda: block_copy(ACROSS, src, c).wait_recv())
         when(both(early(c), goes_up(c, False)), lambda: block_copy(UP, src, c).start())
         when(both(early(c), goes_down(c, False)), lambda: block_copy(DOWN, src, c).start())
 
@@ -330,9 +374,10 @@
             (UP, z - d, goes_up, z - d >= 0),
         )
 
-    def line(c, d):
+    def line(i, k, d):
         for way, ahead, more, there in ways(d):
             src = ahead * 2 + y
+            c = order(way, k)
 
             @pl.when(there)
             def _():
@@ -342,57 +387,102 @@
                     both(no(early(c)), owner(c) != other), lambda: block_copy(ACROSS, src, c).start()
                 )
 
-    def far_line(c, d):
+    def take_far(i, src, c):
+        when(
+            jnp.logical_or(owner(c) != r, i <= STATS_AT),
+            lambda: block_copy(ACROSS, src, c).wait_recv(),
+        )
+
+    def early_line(i, d):
         for way, ahead, more, there in ways(d):
             src = ahead * 2 + 1 - y
 
             @pl.when(there)
             def _():
-                when(owner(c) != r, lambda: block_copy(ACROSS, src, c).wait_recv())
-                when(both(early(c), more(c, False)), lambda: block_copy(way, src, c).start())
-
-    def drain(c):
-        for src_z in range(nz):
-            for src_y in range(2):
-                src = src_z * 2 + src_y
-                on_line = src_y == y
-                up = jnp.where(on_line, goes_up(c, True), both(early(c), goes_up(c, False)))
-                down = jnp.where(on_line, goes_down(c, True), both(early(c), goes_down(c, False)))
-                kept = both(src_z != z, both(early(c), owner(c) != other))
-                when(both(up, src_z <= z), lambda: block_copy(UP, src, c).wait_send())
-                when(both(down, src_z >= z), lambda: block_copy(DOWN, src, c).wait_send())
-                when(both(on_line, no(kept)), lambda: block_copy(ACROSS, src, c).wait_send())
+                for c in EARLY:
+                    take_far(i, src, c)
+                    when(more(c, False), lambda: block_copy(way, src, c).start())
+
+    def far_line(i, k, d):
+        for way, ahead, more, there in ways(d):
+            c = order(way, k)
+            when(both(there, no(early(c))), lambda: take_far(i, ahead * 2 + 1 - y, c))
+
+    def drain(k):
+        across = order(ACROSS, k)
+        block_copy(ACROSS, r, across).wait_send()
+        for way in (DOWN, UP):
+            c = order(way, k)
+            for d in range(nz):
+                ahead = z + d if way == DOWN else z - d
+                more = goes_down(c, True) if way == DOWN else goes_up(c, True)
+                there = ahead < nz if way == DOWN else ahead >= 0
+
+                @pl.when(there)
+                def _():
+                    src = ahead * 2 + y
+                    when(more, lambda: block_copy(way, src, c).wait_send())
+                    if d > 0:
+                        when(
+                            jnp.logical_or(no(early(c)), owner(c) == other),
+                            lambda: block_copy(ACROSS, src, c).wait_send(),
+                        )
+
+    def drain_early():
+        for c in EARLY:
+            for way in (DOWN, UP):
+                for d in range(nz):
+                    ahead = z + d if way == DOWN else z - d
+                    more = goes_down(c, False) if way == DOWN else goes_up(c, False)
+                    there = ahead < nz if way == DOWN else ahead >= 0
+                    src = ahead * 2 + 1 - y
+                    when(both(there, more), lambda: block_copy(way, src, c).wait_send())
+
+    middle = both(z > 0, z < nz - 1)
+
+    def ready(i):
+        last = i - nz + 2
+        return jnp.where(middle, 2 * last - chunks, last)
 
     def done_by(i):
-        return jnp.clip(jnp.minimum((i - first + 1) * pace, i - nz + 2), 0, chunks)
+        return jnp.clip(jnp.minimum((i - first + 1) * pace, ready(i)), 0, chunks)
+
+    def nth(k):
+        half = chunks // 2
+        inner = jnp.where(k % 2 == 0, half - 1 - k // 2, half + k // 2)
+        return jnp.where(middle, inner, jnp.where(z == 0, chunks - 1 - k, k))
 
     def step_of(i, carry):
-        when(i + LEAD < chunks, lambda: send_own(i + LEAD))
+        for way in (DOWN, UP):
+            own_line(way, i + lead(way))
+        own_across(i + LEAD_Y)
         when(i < chunks, lambda: beside(i))
+        hooks(i, 0)
         for d in range(1, nz):
-            c = i - (d - 1)
-            when(both(c >= 0, c < chunks), lambda: line(c, d))
+            k = i - (d - 1)
+            when(both(k >= 0, k < chunks), lambda: line(i, k, d))
+            if d < nz - 1:
+                hooks(i, d)
         for d in range(1, nz):
-            c = i - d
-            when(both(both(c >= 0, c < chunks), early(c)), lambda: far_line(c, d))
+            when(i == EARLY_AT + d, lambda: early_line(i, d))
         last = i - (nz - 1)
 
-        @pl.when(both(last >= 0, no(early(last))))
+        @pl.when(last >= 0)
         def _():
             for d in range(1, nz):
-                far_line(last, d)
-
-        for at, stage in stages.items():
-            when(i == at, stage)
-
-        def output(c, carry):
-            make_output(c)
+                far_line(i, last, d)
+
+        hooks(i, 3)
+
+        def output(k, carry):
+            make_output(nth(k))
             return carry
 
         lax.fori_loop(done_by(i - 1), done_by(i), output, 0)
         when(last >= LAG, lambda: drain(last - LAG))
         return carry
 
+    relay()
     steps = chunks + nz - 1
     lax.fori_loop(0, steps, step_of, 0)
 
@@ -415,6 +505,7 @@
         return carry
 
     lax.fori_loop(chunks - LAG, chunks, rest, 0)
+    drain_early()
 
 
 def finish(blocks_ref, out_ref, out_sem):
@@ -487,7 +578,7 @@
             dma((n_rows,)),
         ],
         compiler_params=pltpu.CompilerParams(
-            collective_id=0, has_side_effects=True, vmem_limit_bytes=56 * 1024 * 1024
+            collective_id=0, has_side_effects=True, vmem_limit_bytes=46 * 1024 * 1024
         ),
     )(features.T, prototypes.T, masked_index[None, :])
     return pl.pallas_call(

time: 139 us -> 117 us (0.84)
  Pallas kernels: 135 us -> 114 us
    pallas_call x1, Pallas kernels: 132 us -> 111 us  [with_kernel(): pl.pallas_call(functools.partial(kernel, n_rows, n_protos, masked, protos...]
where the time goes in v2:
time: 117 us
  Pallas kernels  114 us (97%)
  local copies, waits for them, and re-layouts  2.7 us (2%)
    pallas_call x1, Pallas kernels, with_kernel(): pl.pallas_call(functools.partial(kernel, n_rows, n_protos, masked, protos...  111 us
    pallas_call x1, Pallas kernels, with_kernel(): pl.pallas_call(finish, out_shape=jax.ShapeDtypeStruct((rows, total), bf16...  2.74 us
    unnamed x6, local copies, waits for them, and re-layouts  2.7 us

profile of v2, /device:TPU:4, one launch (start us, length us, event | category | flops | bytes accessed | tf_op | source)
XLA Modules:
  0.0 116.5 jit_solution(374524349723348333)
XLA Ops:
  0.0 0.0 copy-start
  0.0 1.2 %copy-done = bf16[16384,32]{0,1:T(8,128)(2,1)S(1)} copy-done((bf16[16384,32]{0,1:T(8,128)(2,1)S(1)}, bf16[16384,32]{0,1:T(8,128)(2,1)}, u32[]{:S(2)}) %copy-start) | copy-done | bytes 1048600
  1.2 0.0 copy-start.1
  1.2 0.8 copy-done.1
  2.0 0.0 copy-start.2
  2.0 0.7 copy-done.2
  2.7 111.1 %shard_map.37.blocks_ref = bf16[8,192,2048]{2,1,0:T(8,128)(2,1)S(1)} custom-call(bf16[64,384]{1,0:T(8,128)(2,1)S(1)} %bitcast.4, bf16[32,16384]{1,0:T(8,128)(2,1)S(1)} %bitcast.3, s32[1,192]{1,0:T(1,128)S(1)} %bitcast.5), custom_call_target="tpu_custom_call" | custom-call | tf_op jit(solution)/shard_map/pallas_call | solution.py:539
  113.8 2.7 %shard_map.38 = bf16[192,16384]{1,0:T(8,128)(2,1)} custom-call(bf16[8,192,2048]{2,1,0:T(8,128)(2,1)S(1)} %shard_map.37.blocks_ref), custom_call_target="tpu_custom_call" | custom-call | tf_op jit(solution)/shard_map/pallas_call | solution.py:584
Async XLA Ops:
  0.0 1.2 %copy-start = (bf16[16384,32]{0,1:T(8,128)(2,1)S(1)}, bf16[16384,32]{0,1:T(8,128)(2,1)}, u32[]{:S(2)}) copy-start(bf16[16384,32]{0,1:T(8,128)(2,1)} %param.4) | copy-start | bytes 3145732
  1.2 0.8 copy-start.1
  2.0 0.7 copy-start.2

commit v3 on v2

--- a/solution.py
+++ b/solution.py
@@ -16,6 +16,8 @@
 UP, DOWN, ACROSS = 0, 1, 2
 LEAD_Z = (8, 3, 6, 0)
 LEAD_Y = 8
+FIRST_Z = 1
+FIRST_Y = 1
 SPLIT = 1
 EARLY = (4,)
 EARLY_AT = 3
@@ -29,7 +31,7 @@
     feat_ref, proto_ref, index_ref, out_ref,
     feat_in, index, onehot, picks, patches, pair, chosen, lane_scale, feat_scale, full, weights,
     acc, row_out, row_in, mass_out, mass_in, row_scale, out_scale, scales,
-    in_sem, own_sem, pick_send, pick_recv, patch_send, patch_recv, send, recv, direct_send,
+    line_sem, in_sem, own_sem, pick_send, pick_recv, patch_send, patch_recv, send, recv, direct_send,
     row_send, row_recv, mass_send, mass_recv, scale_send, scale_recv,
 ):
     r, p = lax.axis_index("rows"), lax.axis_index("protos")
@@ -105,11 +107,12 @@
 
     def pick_copy(step):
         return remote(
-            picks.at[r], picks.at[r], pick_send.at[step], pick_recv.at[r], rows=lax.rem(r + step, n_rows)
-        )
-
-    def pick_from(src):
-        return remote(picks.at[src], picks.at[src], pick_send.at[0], pick_recv.at[src], rows=other)
+            picks.at[y, z], picks.at[y, z], pick_send.at[step], pick_recv.at[z],
+            rows=lax.rem(r + 2 * step, n_rows),
+        )
+
+    def picks_across(column):
+        return remote(picks.at[column], picks.at[column], pick_send.at[0], pick_recv.at[nz], rows=other)
 
     def patch_copy(step, src):
         part = patches.at[pl.ds(pl.multiple_of(src * fdim, fdim), fdim)]
@@ -142,14 +145,15 @@
     each(chunks, lambda c: own_copy(c).start())
 
     barrier = pltpu.get_barrier_semaphore()
-    for step in range(1, n_rows):
-        pl.semaphore_signal(
-            barrier, inc=1, device_id={"rows": lax.rem(r + step, n_rows)}, device_id_type=mesh_id
-        )
+
+    def greet(semaphore, **device):
+        pl.semaphore_signal(semaphore, inc=1, device_id=device, device_id_type=mesh_id)
+
+    greet(barrier, rows=other)
+    when(z > 0, lambda: greet(barrier, rows=r - 2))
+    when(z < nz - 1, lambda: greet(barrier, rows=r + 2))
     for step in range(1, n_protos):
-        pl.semaphore_signal(
-            barrier, inc=1, device_id={"protos": lax.rem(p + step, n_protos)}, device_id_type=mesh_id
-        )
+        greet(barrier, protos=lax.rem(p + step, n_protos))
 
     onehot[...] = jnp.zeros_like(onehot)
     index_load.wait()
@@ -158,24 +162,9 @@
     feat_load.wait()
     picked = jnp.dot(feat_in[...], onehot[...], preferred_element_type=jnp.float32)
     picked = jnp.where(odd, pltpu.roll(picked, 2 * BLOCK - rows, 1), picked)
-    picks[r] = picked.astype(jnp.bfloat16)
+    picks[y, z] = picked.astype(jnp.bfloat16)
     acc[...] = jnp.zeros_like(acc)
     each(chunks, lambda c: own_copy(c).wait())
-
-    pl.semaphore_wait(barrier, n_rows + n_protos - 2)
-
-    for step in range(1, n_rows):
-        pick_copy(step).start()
-
-    def begin(c):
-        when(both(owner(c) == other, c >= 0), lambda: block_copy(ACROSS, r, c).start())
-
-    each(chunks, begin)
-    for apart in range(1, nz):
-        for side in (1, -1):
-            there = both(z + side * apart >= 0, z + side * apart < nz)
-            for c in range(2 * SPLIT):
-                when(there, lambda: direct_copy(lax.rem(nz + side * apart, nz), c).start())
 
     def order(way, k):
         if way == ACROSS:
@@ -199,20 +188,62 @@
         c = order(ACROSS, k)
         when(both(k < chunks, owner(c) != other), lambda: block_copy(ACROSS, r, c).start())
 
+    def hear(sem, behind, ahead_there, ahead):
+        when(behind, lambda: pl.semaphore_wait(sem, 1))
+        when(ahead_there, lambda: greet(sem, rows=ahead))
+
+    def hear_up():
+        hear(line_sem.at[UP], z > 0, z < nz - 1, r + 2)
+
+    def hear_down():
+        hear(line_sem.at[DOWN], z < nz - 1, z > 0, r - 2)
+
+    met = n_protos - 1 + 1 + jnp.where(z > 0, 1, 0) + jnp.where(z < nz - 1, 1, 0)
+    pl.semaphore_wait(barrier, met)
     for way in (DOWN, UP):
-        each(lead(way), functools.partial(own_line, way))
-    each(LEAD_Y, own_across)
-
-    for step in range(1, n_rows):
-        pick_from(lax.rem(r + step, n_rows)).wait_recv()
+        for k in range(FIRST_Z):
+            own_line(way, k)
+    for j in range(SPLIT):
+        block_copy(ACROSS, r, other * SPLIT + j).start()
+    for k in range(FIRST_Y):
+        own_across(k)
+
+    @pl.when(z < nz // 2)
+    def _():
+        hear_up()
+        hear_down()
+
+    @pl.when(z >= nz // 2)
+    def _():
+        hear_down()
+        hear_up()
+
+    for step in range(1, nz):
+        pick_copy(step).start()
+    for apart in range(1, nz):
+        for side in (1, -1):
+            there = both(z + side * apart >= 0, z + side * apart < nz)
+            for c in range(2 * SPLIT):
+                when(there, lambda: direct_copy(lax.rem(nz + side * apart, nz), c).start())
+    for way in (DOWN, UP):
+        each(lead(way) - FIRST_Z, lambda k: own_line(way, k + FIRST_Z))
+
+    for step in range(1, nz):
+        src = lax.rem(z + step, nz)
+        remote(
+            picks.at[y, src], picks.at[y, src], pick_send.at[0], pick_recv.at[src], rows=other
+        ).wait_recv()
+    picks_across(y).start()
+    each(LEAD_Y - FIRST_Y, lambda k: own_across(k + FIRST_Y))
+    picks_across(1 - y).wait_recv()
     mine = pl.ds(pl.multiple_of(p * fdim, fdim), fdim)
     for j in range(nz):
         at = 3 * BLOCK * j
-        patches[mine, at:at + BLOCK] = picks[2 * j, :, :BLOCK]
+        patches[mine, at:at + BLOCK] = picks[0, j, :, :BLOCK]
         patches[mine, at + BLOCK:at + 2 * BLOCK] = (
-            picks[2 * j, :, BLOCK:].astype(jnp.float32) + picks[2 * j + 1, :, :BLOCK].astype(jnp.float32)
+            picks[0, j, :, BLOCK:].astype(jnp.float32) + picks[1, j, :, :BLOCK].astype(jnp.float32)
         ).astype(jnp.bfloat16)
-        patches[mine, at + 2 * BLOCK:at + 3 * BLOCK] = picks[2 * j + 1, :, BLOCK:]
+        patches[mine, at + 2 * BLOCK:at + 3 * BLOCK] = picks[1, j, :, BLOCK:]
     for step in range(1, n_protos):
         patch_copy(step, p).start()
 
@@ -486,8 +517,10 @@
     steps = chunks + nz - 1
     lax.fori_loop(0, steps, step_of, 0)
 
+    picks_across(y).wait_send()
+    for step in range(1, nz):
+        pick_copy(step).wait_send()
     for step in range(1, n_rows):
-        pick_copy(step).wait_send()
         scale_copy(step, r).wait_send()
     for step in range(1, nz):
         for c in range(2 * SPLIT):
@@ -545,7 +578,7 @@
             pltpu.VMEM((fdim, patches), bf16),
             pltpu.VMEM((1, rows), jnp.int32),
             pltpu.VMEM((patches, 2 * BLOCK), bf16),
-            pltpu.VMEM((n_rows, fdim, 2 * BLOCK), bf16),
+            pltpu.VMEM((2, n_rows // 2, fdim, 2 * BLOCK), bf16),
             pltpu.VMEM((depth, lanes), bf16),
             pltpu.VMEM((2 * rows, depth), bf16),
             pltpu.VMEM((rows, depth), bf16),
@@ -561,6 +594,7 @@
             pltpu.VMEM((1, lanes), f32),
             pltpu.VMEM((rows, BLOCK), f32),
             pltpu.VMEM((n_rows, 2, 1, width), f32),
+            pltpu.SemaphoreType.REGULAR((2,)),
             dma((2,)),
             dma((chunks,)),
             dma((n_rows,)),
@@ -580,7 +614,7 @@
         compiler_params=pltpu.CompilerParams(
             collective_id=0, has_side_effects=True, vmem_limit_bytes=46 * 1024 * 1024
         ),
-    )(features.T, prototypes.T, masked_index[None, :])
+    )(*(pltpu.with_memory_space_constraint(x, pltpu.HBM) for x in (features.T, prototypes.T, masked_index[None, :])))
     return pl.pallas_call(
         finish,
         out_shape=jax.ShapeDtypeStruct((rows, total), bf16),

time: 117 us -> 111 us (0.949)
  Pallas kernels: 114 us -> 111 us
  local copies, waits for them, and re-layouts: 2.7 us -> 0 us
    unnamed x6 -> x0, local copies, waits for them, and re-layouts: 2.7 us -> none
    pallas_call x1, Pallas kernels: 111 us -> 108 us  [with_kernel(): pl.pallas_call(functools.partial(kernel, n_rows, n_protos, masked, protos...]
where the time goes in v3:
time: 111 us
  Pallas kernels  111 us (100%)
    pallas_call x1, Pallas kernels, with_kernel(): pl.pallas_call(functools.partial(kernel, n_rows, n_protos, masked, protos...  108 us
    pallas_call x1, Pallas kernels, with_kernel(): pl.pallas_call(finish, out_shape=jax.ShapeDtypeStruct((rows, total), bf16...  2.74 us

profile of v3, /device:TPU:4, one launch (start us, length us, event | category | flops | bytes accessed | tf_op | source)
XLA Modules:
  0.0 111.2 jit_solution(15987215415279187652)
XLA Ops:
  0.0 108.4 %shard_map.37.blocks_ref = bf16[8,192,2048]{2,1,0:T(8,128)(2,1)S(1)} custom-call(bf16[64,384]{1,0:T(8,128)(2,1)} %bitcast.4, bf16[32,16384]{1,0:T(8,128)(2,1)} %bitcast.3, s32[1,192]{1,0:T(1,128)} %bitcast.5), custom_call_target="tpu_custom_call" | custom-call | tf_op jit(solution)/shard_map/pallas_call | solution.py:572
  108.4 2.7 %shard_map.38 = bf16[192,16384]{1,0:T(8,128)(2,1)} custom-call(bf16[8,192,2048]{2,1,0:T(8,128)(2,1)S(1)} %shard_map.37.blocks_ref), custom_call_target="tpu_custom_call" | custom-call | tf_op jit(solution)/shard_map/pallas_call | solution.py:618

commit v4 on v3

--- a/solution.py
+++ b/solution.py
@@ -17,19 +17,22 @@
 LEAD_Z = (8, 3, 6, 0)
 LEAD_Y = 8
 FIRST_Z = 1
-FIRST_Y = 1
+FIRST_Y = 2
 SPLIT = 1
 EARLY = (4,)
 EARLY_AT = 3
 LAG = 2
-STATS_AT = 0
+STATS_AT = 1
+STAGES = (3, 3, 6, 7, 8, 9, 11, 15, 17, 22, 24, 28)
 BLOCK = 128
+TILE = 256
+PARTS = 2
 
 
 def kernel(
     n_rows, n_protos, masked, protos_all,
     feat_ref, proto_ref, index_ref, out_ref,
-    feat_in, index, onehot, picks, patches, pair, chosen, lane_scale, feat_scale, full, weights,
+    feat_in, index, onehot, picks, pairs, patches, pair, chosen, lane_scale, feat_scale, full, weights,
     acc, row_out, row_in, mass_out, mass_in, row_scale, out_scale, scales,
     line_sem, in_sem, own_sem, pick_send, pick_recv, patch_send, patch_recv, send, recv, direct_send,
     row_send, row_recv, mass_send, mass_recv, scale_send, scale_recv,
@@ -105,14 +108,14 @@
             where(r, chunk), where(r, chunk), direct_send.at[step, c], recv.at[r, chunk], rows=target
         )
 
-    def pick_copy(step):
+    def pick_across():
+        return remote(picks.at[0], picks.at[1], pick_send.at[0], pick_recv.at[nz], rows=other)
+
+    def pick_copy(step, src):
         return remote(
-            picks.at[y, z], picks.at[y, z], pick_send.at[step], pick_recv.at[z],
+            pairs.at[src], pairs.at[src], pick_send.at[step], pick_recv.at[src],
             rows=lax.rem(r + 2 * step, n_rows),
         )
-
-    def picks_across(column):
-        return remote(picks.at[column], picks.at[column], pick_send.at[0], pick_recv.at[nz], rows=other)
 
     def patch_copy(step, src):
         part = patches.at[pl.ds(pl.multiple_of(src * fdim, fdim), fdim)]
@@ -162,7 +165,7 @@
     feat_load.wait()
     picked = jnp.dot(feat_in[...], onehot[...], preferred_element_type=jnp.float32)
     picked = jnp.where(odd, pltpu.roll(picked, 2 * BLOCK - rows, 1), picked)
-    picks[y, z] = picked.astype(jnp.bfloat16)
+    picks[0] = picked.astype(jnp.bfloat16)
     acc[...] = jnp.zeros_like(acc)
     each(chunks, lambda c: own_copy(c).wait())
 
@@ -200,6 +203,7 @@
 
     met = n_protos - 1 + 1 + jnp.where(z > 0, 1, 0) + jnp.where(z < nz - 1, 1, 0)
     pl.semaphore_wait(barrier, met)
+    pick_across().start()
     for way in (DOWN, UP):
         for k in range(FIRST_Z):
             own_line(way, k)
@@ -218,8 +222,16 @@
         hear_down()
         hear_up()
 
+    pick_across().wait()
+    mine = picks[0].astype(jnp.float32)
+    theirs = picks[1].astype(jnp.float32)
+    even = jnp.where(odd, theirs, mine)
+    uneven = jnp.where(odd, mine, theirs)
+    pairs[z, :, :BLOCK] = even[:, :BLOCK].astype(jnp.bfloat16)
+    pairs[z, :, BLOCK:2 * BLOCK] = (even[:, BLOCK:] + uneven[:, :BLOCK]).astype(jnp.bfloat16)
+    pairs[z, :, 2 * BLOCK:] = uneven[:, BLOCK:].astype(jnp.bfloat16)
     for step in range(1, nz):
-        pick_copy(step).start()
+        pick_copy(step, z).start()
     for apart in range(1, nz):
         for side in (1, -1):
             there = both(z + side * apart >= 0, z + side * apart < nz)
@@ -228,24 +240,16 @@
     for way in (DOWN, UP):
         each(lead(way) - FIRST_Z, lambda k: own_line(way, k + FIRST_Z))
 
-    for step in range(1, nz):
-        src = lax.rem(z + step, nz)
-        remote(
-            picks.at[y, src], picks.at[y, src], pick_send.at[0], pick_recv.at[src], rows=other
-        ).wait_recv()
-    picks_across(y).start()
     each(LEAD_Y - FIRST_Y, lambda k: own_across(k + FIRST_Y))
-    picks_across(1 - y).wait_recv()
-    mine = pl.ds(pl.multiple_of(p * fdim, fdim), fdim)
-    for j in range(nz):
-        at = 3 * BLOCK * j
-        patches[mine, at:at + BLOCK] = picks[0, j, :, :BLOCK]
-        patches[mine, at + BLOCK:at + 2 * BLOCK] = (
-            picks[0, j, :, BLOCK:].astype(jnp.float32) + picks[1, j, :, :BLOCK].astype(jnp.float32)
-        ).astype(jnp.bfloat16)
-        patches[mine, at + 2 * BLOCK:at + 3 * BLOCK] = picks[1, j, :, BLOCK:]
-    for step in range(1, n_protos):
-        patch_copy(step, p).start()
+
+    def spread_picks():
+        for step in range(1, nz):
+            pick_copy(step, lax.rem(z + step, nz)).wait_recv()
+        mine = pl.ds(pl.multiple_of(p * fdim, fdim), fdim)
+        for j in range(nz):
+            patches[mine, 3 * BLOCK * j:3 * BLOCK * (j + 1)] = pairs[j]
+        for step in range(1, n_protos):
+            patch_copy(step, p).start()
 
     def relay():
         for apart in range(1, nz):
@@ -288,34 +292,38 @@
     def turned(column):
         return jnp.broadcast_to(column, (BLOCK, BLOCK)).T[:1]
 
-    def add_rows(value, col_mass, tile):
+    def add_rows(value, col_mass):
         col_scale = 1.0 / (protos_all * col_mass)
-        scaled = (value * col_scale).reshape(BLOCK // 8, 8, lanes)
+        scaled = (value * col_scale).reshape(value.shape[0] // 8, 8, lanes)
         acc[...] += jnp.sum(scaled, axis=0)
         return col_scale
 
-    def make_weights(half):
+    def make_weights(part):
+        count = width // TILE // PARTS
+
         def body(i):
-            tile = half * (width // BLOCK // 2) + i
-            per = span // BLOCK
-            within = pl.ds(pl.multiple_of(lax.rem(tile, per) * BLOCK, BLOCK), BLOCK)
+            tile = part * count + i
+            per = span // TILE
+            within = pl.ds(pl.multiple_of(lax.rem(tile, per) * TILE, TILE), TILE)
             block = full[r * SPLIT + tile // per, :, within].T
             wide = block.astype(jnp.float32)
             proto_scale = lax.rsqrt(jnp.sum(wide * wide, axis=1, keepdims=True) + EPS)
             raw = jnp.dot(block, patches[...], preferred_element_type=jnp.float32)
             value = jnp.exp2(raw * lane_scale[...] * proto_scale)
-            weights[pl.ds(pl.multiple_of(tile * BLOCK, BLOCK), BLOCK)] = value
-            add_rows(value, jnp.sum(value, axis=1, keepdims=True), tile)
-            scales[r, 1, :, pl.ds(pl.multiple_of(tile * BLOCK, BLOCK), BLOCK)] = turned(proto_scale)
-
-        each(width // BLOCK // 2, body)
+            weights[pl.ds(pl.multiple_of(tile * TILE, TILE), TILE)] = value
+            add_rows(value, jnp.sum(value, axis=1, keepdims=True))
+            for j in range(TILE // BLOCK):
+                at = pl.ds(pl.multiple_of(tile * TILE + j * BLOCK, BLOCK), BLOCK)
+                scales[r, 1, :, at] = turned(proto_scale[j * BLOCK:(j + 1) * BLOCK])
+
+        each(count, body)
 
     def one_pass(it):
         def body(tile):
             at = pl.ds(pl.multiple_of(tile * BLOCK, BLOCK), BLOCK)
             value = weights[at]
             col_mass = jnp.sum(value * row_scale[...], axis=1, keepdims=True)
-            col_scale = add_rows(value, col_mass, tile)
+            col_scale = add_rows(value, col_mass)
             if it == ITERS - 1:
                 scales[r, 0, :, at] = turned(col_scale)
 
@@ -371,24 +379,26 @@
             value = out_scale[:, :1] * value * scales[owner(c), 0, :, at]
             out_ref[c, :, t * tile:(t + 1) * tile] = value.astype(jnp.bfloat16)
 
-    stages = {
-        (0, 2): take_patches,
-        (STATS_AT, 3): take_own,
-        (1, 0): lambda: make_weights(0),
-        (1, 2): lambda: (make_weights(1), give_rows(0)),
-        (1, 3): lambda: give_mass(0),
-        (2, 3): lambda: next_pass(1),
-        (3, 1): lambda: give_mass(1),
-        (4, 2): lambda: next_pass(2),
-        (4, 3): lambda: give_mass(2),
-        (6, 1): settle,
-    }
-    first = 6
+    work = (
+        spread_picks,
+        relay,
+        take_patches,
+        take_own,
+        lambda: make_weights(0),
+        lambda: (make_weights(1), give_rows(0)),
+        lambda: give_mass(0),
+        lambda: next_pass(1),
+        lambda: give_mass(1),
+        lambda: next_pass(2),
+        lambda: give_mass(2),
+        settle,
+    )
+    first = (STAGES[-1] + 1) // 4
 
     def hooks(i, place):
-        for (at, position), stage in stages.items():
-            if position == place:
-                when(i == at, stage)
+        for at, stage in zip(STAGES, work):
+            if at % 4 == place:
+                when(i == at // 4, stage)
 
     pace = 4
 
@@ -472,7 +482,7 @@
     middle = both(z > 0, z < nz - 1)
 
     def ready(i):
-        last = i - nz + 2
+        last = i - nz + 1
         return jnp.where(middle, 2 * last - chunks, last)
 
     def done_by(i):
@@ -482,6 +492,10 @@
         half = chunks // 2
         inner = jnp.where(k % 2 == 0, half - 1 - k // 2, half + k // 2)
         return jnp.where(middle, inner, jnp.where(z == 0, chunks - 1 - k, k))
+
+    def output(k, carry):
+        make_output(nth(k))
+        return carry
 
     def step_of(i, carry):
         for way in (DOWN, UP):
@@ -494,6 +508,8 @@
             when(both(k >= 0, k < chunks), lambda: line(i, k, d))
             if d < nz - 1:
                 hooks(i, d)
+            if d == nz - 2:
+                lax.fori_loop(done_by(i - 1), done_by(i), output, 0)
         for d in range(1, nz):
             when(i == EARLY_AT + d, lambda: early_line(i, d))
         last = i - (nz - 1)
@@ -505,21 +521,15 @@
 
         hooks(i, 3)
 
-        def output(k, carry):
-            make_output(nth(k))
-            return carry
-
-        lax.fori_loop(done_by(i - 1), done_by(i), output, 0)
         when(last >= LAG, lambda: drain(last - LAG))
         return carry
 
-    relay()
     steps = chunks + nz - 1
     lax.fori_loop(0, steps, step_of, 0)
-
-    picks_across(y).wait_send()
+    lax.fori_loop(done_by(steps - 1), chunks, output, 0)
+
     for step in range(1, nz):
-        pick_copy(step).wait_send()
+        pick_copy(step, z).wait_send()
     for step in range(1, n_rows):
         scale_copy(step, r).wait_send()
     for step in range(1, nz):
@@ -578,7 +588,8 @@
             pltpu.VMEM((fdim, patches), bf16),
             pltpu.VMEM((1, rows), jnp.int32),
             pltpu.VMEM((patches, 2 * BLOCK), bf16),
-            pltpu.VMEM((2, n_rows // 2, fdim, 2 * BLOCK), bf16),
+            pltpu.VMEM((2, fdim, 2 * BLOCK), bf16),
+            pltpu.VMEM((n_rows // 2, fdim, 3 * BLOCK), bf16),
             pltpu.VMEM((depth, lanes), bf16),
             pltpu.VMEM((2 * rows, depth), bf16),
             pltpu.VMEM((rows, depth), bf16),

time: 111 us -> 106 us (0.955)
  Pallas kernels: 111 us -> 106 us
    pallas_call x1, Pallas kernels: 108 us -> 103 us  [with_kernel(): pl.pallas_call(functools.partial(kernel, n_rows, n_protos, masked, protos...]
where the time goes in v4:
time: 106 us
  Pallas kernels  106 us (100%)
    pallas_call x1, Pallas kernels, with_kernel(): pl.pallas_call(functools.partial(kernel, n_rows, n_protos, masked, protos...  103 us
    pallas_call x1, Pallas kernels, with_kernel(): pl.pallas_call(finish, out_shape=jax.ShapeDtypeStruct((rows, total), bf16...  2.74 us

profile of v4, /device:TPU:4, one launch (start us, length us, event | category | flops | bytes accessed | tf_op | source)
XLA Modules:
  0.0 106.2 jit_solution(12447363699070984407)
XLA Ops:
  0.0 103.4 %shard_map.37.blocks_ref = bf16[8,192,2048]{2,1,0:T(8,128)(2,1)S(1)} custom-call(bf16[64,384]{1,0:T(8,128)(2,1)} %bitcast.4, bf16[32,16384]{1,0:T(8,128)(2,1)} %bitcast.3, s32[1,192]{1,0:T(1,128)} %bitcast.5), custom_call_target="tpu_custom_call" | custom-call | tf_op jit(solution)/shard_map/pallas_call | solution.py:582
  103.4 2.7 %shard_map.38 = bf16[192,16384]{1,0:T(8,128)(2,1)} custom-call(bf16[8,192,2048]{2,1,0:T(8,128)(2,1)S(1)} %shard_map.37.blocks_ref), custom_call_target="tpu_custom_call" | custom-call | tf_op jit(solution)/shard_map/pallas_call | solution.py:629

commit v5 on v4

--- a/solution.py
+++ b/solution.py
@@ -14,7 +14,7 @@
 EPS = 1e-06
 LOG2E = 1.4426950408889634
 UP, DOWN, ACROSS = 0, 1, 2
-LEAD_Z = (8, 3, 6, 0)
+LEAD_Z = (3, 2, 4, 0)
 LEAD_Y = 8
 FIRST_Z = 1
 FIRST_Y = 2
@@ -23,9 +23,9 @@
 EARLY_AT = 3
 LAG = 2
 STATS_AT = 1
-STAGES = (3, 3, 6, 7, 8, 9, 11, 15, 17, 22, 24, 28)
+STAGES = (3, 3, 6, 7, 8, 9, 11, 15, 17, 21, 23, 28)
 BLOCK = 128
-TILE = 256
+TILE = 512
 PARTS = 2
 
 

time: 106 us -> 106 us (level)
  no operation moved by 1% of the time
where the time goes in v5:
time: 106 us
  Pallas kernels  106 us (100%)
    pallas_call x1, Pallas kernels, with_kernel(): pl.pallas_call(functools.partial(kernel, n_rows, n_protos, masked, protos...  103 us
    pallas_call x1, Pallas kernels, with_kernel(): pl.pallas_call(finish, out_shape=jax.ShapeDtypeStruct((rows, total), bf16...  2.74 us

profile of v5, /device:TPU:4, one launch (start us, length us, event | category | flops | bytes accessed | tf_op | source)
XLA Modules:
  0.0 105.6 jit_solution(15551537901801670417)
XLA Ops:
  0.0 102.8 %shard_map.37.blocks_ref = bf16[8,192,2048]{2,1,0:T(8,128)(2,1)S(1)} custom-call(bf16[64,384]{1,0:T(8,128)(2,1)} %bitcast.4, bf16[32,16384]{1,0:T(8,128)(2,1)} %bitcast.3, s32[1,192]{1,0:T(1,128)} %bitcast.5), custom_call_target="tpu_custom_call" | custom-call | tf_op jit(solution)/shard_map/pallas_call | solution.py:582
  102.8 2.7 %shard_map.38 = bf16[192,16384]{1,0:T(8,128)(2,1)} custom-call(bf16[8,192,2048]{2,1,0:T(8,128)(2,1)S(1)} %shard_map.37.blocks_ref), custom_call_target="tpu_custom_call" | custom-call | tf_op jit(solution)/shard_map/pallas_call | solution.py:629
